TPU v7x, 32 devices: a whole 2x2x4 slice. The times are simulated.
32 devices in a mesh: pq: 2 (over x), rs: 16 (over z, y, core).
Axes of the slice: x: 2, y: 2, z: 4, core: 2. Of those that a mesh axis runs over, the one named last changes fastest.
Arguments:
- integrals: bfloat16 [128, 1152, 1152], P('pq', 'rs'), may hold values from -6 to 6
- coeff: bfloat16 [1152, 896], P('rs', 'pq'), may hold values from -0.1875 to 0.1875
Outputs:
- half_mo: bfloat16 [128, 896, 896], P('pq', 'rs')
All inputs are finite; a program needn't handle non-finite values.
Results may differ from a plain program's by a relative error of at most 0.0049.
Values may be sent and summed in bfloat16 or wider, within the bound.
A program may use at most 128 MiB of HBM per device.

v0:
```python
import jax
import jax.numpy as jnp
from jax import lax
from jax.sharding import PartitionSpec as P

NBASIS = 1152
NORB = 896


def second_half(received, panel):
    return jnp.einsum("prl,rk->plk", received, panel, preferred_element_type=jnp.float32).astype(
        jnp.bfloat16
    )


def on_device(integrals, coeff):
    pair_rows = integrals.shape[0]
    block_rows = integrals.shape[1]
    flat = integrals.reshape(pair_rows * block_rows, NBASIS)
    strip = lax.all_gather(coeff, "pq", axis=1, tiled=True)
    panel = lax.all_gather(strip, "rs", axis=0, tiled=True)
    first = jnp.dot(flat, panel, preferred_element_type=jnp.float32).astype(jnp.bfloat16)
    first = first.reshape(pair_rows, block_rows, NORB)
    return second_half(lax.all_to_all(first, "rs", split_axis=2, concat_axis=1, tiled=True), panel)


def solution(mesh):
    placed = (P("pq", "rs", None), P("rs", "pq"))
    return jax.shard_map(
        on_device, mesh=mesh, in_specs=placed, out_specs=P("pq", "rs", None), check_vma=False
    )
```

profile of v0, /device:TPU:1, one launch (start us, length us, event | category | flops | bytes accessed | tf_op | source)
XLA Modules:
  0.0 468.6 jit_solution(1243256376461925950)
XLA Ops:
  6.5 0.0 all-gather.3.cloned.1.call-start
  6.5 4.7 %all-gather = bf16[2,448,72]{1,2,0:T(8,128)(2,1)S(1)} all-gather(bf16[1,448,72]{1,2,0:T(8,128)(2,1)} %bitcast.25), channel_id=1, replica_groups=mesh['pq'=2,'rs'=16] {'pq'}, dimensions={0}, use_global_device_ids=true | all-gather | bytes 193536 | tf_op jit(solution)/shard_map/all_gather | solution.py:20
  11.2 0.1 copy.7
  11.3 0.8 reshape.9
  12.1 0.0 all-gather.3.cloned.1.call-update
  12.2 44.5 %all-gather.3.cloned.1.call-done = bf16[1152,896]{1,0:T(8,128)(2,1)} async-done(((bf16[72,896]{1,0:T(8,128)(2,1)}), bf16[1152,896]{1,0:T(8,128)(2,1)}) %all-gather.3.cloned.1.call-update) | async-done | bytes 2064400 | tf_op jit(solution)/shard_map/all_gather | solution.py:21
  56.7 17.5 %convolution_convert_fusion = bf16[4608,896]{1,0:T(8,128)(2,1)} fusion(bf16[4608,1152]{1,0:T(8,128)(2,1)} %bitcast.26, bf16[1152,896]{1,0:T(8,128)(2,1)} %all-gather.3.cloned.1.call-done), kind=kOutput, calls=%fused_computation | convolution fusion | flops 9516810240 | bytes 20938752 | tf_op jit(solution)/shard_map/dot_general | solution.py:22
  74.2 18.5 %copy.8 = bf16[64,72,896]{1,0,2:T(8,128)(2,1)} copy(bf16[64,72,896]{2,1,0:T(8,128)(2,1)} %bitcast.23) | data formatting | bytes 16515072 | tf_op jit(solution)/shard_map/reshape | solution.py:23
  92.7 321.5 %all_to_all.18 = bf16[64,72,896]{1,0,2:T(8,128)(2,1)S(1)} all-to-all(bf16[64,72,896]{1,0,2:T(8,128)(2,1)} %copy.8), channel_id=1, replica_groups=mesh['pq'=2,'rs'=16] {'rs'}, dimensions={2} | all-to-all | bytes 16515072 | tf_op jit(solution)/shard_map/all_to_all | solution.py:24
  414.1 10.6 %copy.10 = bf16[64,16,72,56]{2,1,3,0:T(8,128)(2,1)} copy(bf16[64,16,72,56]{2,0,3,1:T(8,128)(2,1)S(1)} %bitcast.22) | data formatting | bytes 16515072 | tf_op jit(solution)/shard_map/all_to_all | solution.py:24
  424.7 0.0 copy-start
  424.7 23.2 %all_to_all.16 = bf16[64,1152,56]{1,2,0:T(8,128)(2,1)} reshape(bf16[64,16,72,56]{2,1,3,0:T(8,128)(2,1)} %copy.10) | data formatting | bytes 16515072 | tf_op jit(solution)/shard_map/all_to_all | solution.py:24
  447.9 0.0 copy-done
  447.9 13.8 %convolution_convert_fusion.1 = bf16[64,56,896]{2,1,0:T(8,128)(2,1)} fusion(bf16[64,1152,56]{1,2,0:T(8,128)(2,1)} %all_to_all.16, bf16[1152,896]{1,0:T(8,128)(2,1)S(1)} %copy-done), kind=kOutput, calls=%fused_computation.1 | convolution fusion | flops 7401963520 | bytes 16744448 | tf_op jit(solution)/shard_map/prl,rk->plk/dot_general | solution.py:11
Async XLA Ops:
  6.5 50.2 %all-gather.3.cloned.1.call-start = ((), (), s32[]{:S(2)}) async-start(), calls=%async_computation.1 | async-start | bytes 2193408 | tf_op jit(solution)/shard_map/all_gather | solution.py:21
  424.7 23.2 %copy-start = (bf16[1152,896]{1,0:T(8,128)(2,1)S(1)}, bf16[1152,896]{1,0:T(8,128)(2,1)}, u32[]{:S(2)}) copy-start(bf16[1152,896]{1,0:T(8,128)(2,1)} %all-gather.3.cloned.1.call-done) | copy-start | bytes 6193156
Sparse Core Ops, SparseCore 0:
  12.3 44.3 all-gather.2
where the time goes:
time: 470 us; the launch traced here: 469 us
  blocking collectives  326 us (69%)
  local copies, waits for them, and re-layouts  53.2 us (11%)
  waiting for transfers between devices  44.6 us (9%)
  matrix products  31.3 us (7%)
  between operations  13.4 us (3%)
    all_to_all x1, blocking collectives, on_device(): lax.all_to_all(first, 'rs', split_axis=2, concat_axis=1, tiled=True)  321 us
    all_gather x1, waiting for transfers between devices, on_device(): panel = lax.all_gather(strip, 'rs', axis=0, tiled=True)  44.5 us
    all_to_all x2, local copies, waits for them, and re-layouts, on_device(): lax.all_to_all(first, 'rs', split_axis=2, concat_axis=1, tiled=True)  33.8 us
    reshape x1, local copies, waits for them, and re-layouts, on_device(): first = first.reshape(pair_rows, block_rows, NORB)  18.5 us
    dot_general x1, matrix products, on_device(): jnp.dot(flat, panel, preferred_element_type=jnp.float32)  17.5 us
    dot_general x1, matrix products, second_half(): jnp.einsum('prl,rk->plk', received, panel, preferred_element_type=jnp.flo...  13.8 us
  transfers between devices with their start and end apart: 1, of which 1 were waited for; matrix products, arithmetic and copies ran while one was open for 0% of the time, Pallas kernels for 0%

commit v1 on v0

v1 whole, which is shorter than its diff:
```python
import functools
import math

import jax
import jax.numpy as jnp
from jax import lax
from jax.experimental import pallas as pl
from jax.experimental.pallas import tpu as pltpu
from jax.sharding import PartitionSpec as P

MESH = pl.DeviceIdType.MESH


def second_half(received, panel):
    return jnp.einsum("prl,rk->plk", received, panel, preferred_element_type=jnp.float32).astype(
        jnp.bfloat16
    )


def plain(integrals, panel):
    pair_rows, block_rows, nbasis = integrals.shape
    flat = integrals.reshape(pair_rows * block_rows, nbasis)
    first = jnp.dot(flat, panel, preferred_element_type=jnp.float32).astype(jnp.bfloat16)
    first = first.reshape(pair_rows, block_rows, panel.shape[1])
    return second_half(lax.all_to_all(first, "rs", split_axis=2, concat_axis=1, tiled=True), panel)


def fused_kernel(n, group, x_ref, c_ref, o_ref, tiles, send, recv, stage, load_sem, send_sem, recv_sem, own_sem, out_sem):
    me = lax.axis_index("rs")
    groups = send.shape[0]
    rows = send.shape[2]
    width = stage.shape[2]
    nbasis = tiles.shape[3]
    half = n // 2
    far = lax.rem(me // half + 1, 2) * half
    near = (me // half) * half

    def load(g):
        return pltpu.make_async_copy(x_ref.at[pl.ds(g * group, group)], tiles.at[g % 2], load_sem.at[g % 2])

    def store(g):
        return pltpu.make_async_copy(stage.at[g % 2], o_ref.at[pl.ds(g * group, group)], out_sem.at[g % 2])

    def partner(i):
        if i < half:
            return far + lax.rem(me + i, half)
        return near + lax.rem(me + i - half + 1, half)

    def remote(g, i):
        to = partner(i)
        return pltpu.make_async_remote_copy(
            src_ref=send.at[g, to],
            dst_ref=recv.at[g, me],
            send_sem=send_sem.at[g, i],
            recv_sem=recv_sem.at[g, i],
            device_id={"rs": to},
            device_id_type=MESH,
        )

    def own(g):
        return pltpu.make_async_copy(send.at[g, me], recv.at[g, me], own_sem.at[g])

    load(0).start()
    barrier = pltpu.get_barrier_semaphore()
    for i in range(1, n):
        pl.semaphore_signal(barrier, inc=1, device_id={"rs": lax.rem(me + i, n)}, device_id_type=MESH)
    pl.semaphore_wait(barrier, n - 1)

    step = 4
    for g in range(groups):
        if g + 1 < groups:
            load(g + 1).start()
        load(g).wait()
        for q in range(group // step):
            block = tiles[g % 2, q * step : (q + 1) * step].reshape(step * rows, nbasis)
            first = jnp.dot(block, c_ref[...], preferred_element_type=jnp.float32)
            for j in range(step):
                slot = q * step + j
                piece = first[j * rows : (j + 1) * rows].astype(jnp.bfloat16)
                for d in range(n):
                    send[g, d, :, slot * width : (slot + 1) * width] = piece[:, d * width : (d + 1) * width]
        for i in range(n - 1):
            remote(g, i).start()
        own(g).start()

    for g in range(groups):
        own(g).wait()
        for i in range(n - 1):
            remote(g, i).wait()
        lhs = recv[g].reshape(n * rows, group * width)
        out = lax.dot_general(lhs, c_ref[...], (((0,), (0,)), ((), ())), preferred_element_type=jnp.float32)
        if g >= 2:
            store(g - 2).wait()
        for j in range(group):
            stage[g % 2, j] = out[j * width : (j + 1) * width].astype(jnp.bfloat16)
        store(g).start()
    for g in range(max(groups - 2, 0), groups):
        store(g).wait()


def fused(n, group, integrals, panel):
    pair_rows, rows, nbasis = integrals.shape
    norb = panel.shape[1]
    width = norb // n
    groups = pair_rows // group
    flops = 2 * pair_rows * rows * nbasis * norb + 2 * pair_rows * width * n * rows * norb
    sent = 2 * pair_rows * rows * norb
    return pl.pallas_call(
        functools.partial(fused_kernel, n, group),
        out_shape=jax.ShapeDtypeStruct((pair_rows, width, norb), jnp.bfloat16),
        in_specs=[pl.BlockSpec(memory_space=pl.ANY), pl.BlockSpec(memory_space=pltpu.VMEM)],
        out_specs=pl.BlockSpec(memory_space=pl.ANY),
        scratch_shapes=[
            pltpu.VMEM((2, group, rows, nbasis), jnp.bfloat16),
            pltpu.VMEM((groups, n, rows, group * width), jnp.bfloat16),
            pltpu.VMEM((groups, n, rows, group * width), jnp.bfloat16),
            pltpu.VMEM((2, group, width, norb), jnp.bfloat16),
            pltpu.SemaphoreType.DMA((2,)),
            pltpu.SemaphoreType.DMA((groups, n)),
            pltpu.SemaphoreType.DMA((groups, n)),
            pltpu.SemaphoreType.DMA((groups,)),
            pltpu.SemaphoreType.DMA((2,)),
        ],
        compiler_params=pltpu.CompilerParams(
            collective_id=0, has_side_effects=True, vmem_limit_bytes=60 * 2**20
        ),
        cost_estimate=pl.CostEstimate(flops=flops, bytes_accessed=4 * sent, transcendentals=0),
    )(integrals, panel)


def on_device(n, integrals, coeff):
    pair_rows, rows, nbasis = integrals.shape
    strip = lax.all_gather(coeff, "pq", axis=1, tiled=True)
    panel = lax.all_gather(strip, "rs", axis=0, tiled=True)
    width = panel.shape[1] // n
    group = math.lcm(4, 128 // math.gcd(width, 128))
    if rows % 8 or width % 8 or n % 2 or pair_rows % group or group * width > 2048:
        return plain(integrals, panel)
    return fused(n, group, integrals, panel)


def solution(mesh):
    placed = (P("pq", "rs", None), P("rs", "pq"))
    return jax.shard_map(
        functools.partial(on_device, mesh.shape["rs"]),
        mesh=mesh,
        in_specs=placed,
        out_specs=P("pq", "rs", None),
        check_vma=False,
    )
```

time: 470 us -> 264 us (0.56)
  blocking collectives: 326 us -> 4.69 us
  Pallas kernels: 0 us -> 195 us
  local copies, waits for them, and re-layouts: 53.2 us -> 6.99 us
  matrix products: 31.3 us -> 0 us
    all_to_all x1 -> x0, blocking collectives: 321 us -> none  [on_device(): lax.all_to_all(first, 'rs', split_axis=2, concat_axis=1, tiled=True)]
    pallas_call x0 -> x1, Pallas kernels: none -> 195 us  [fused(): pl.pallas_call(functools.partial(fused_kernel, n, group), out_shape=jax.S...]
    all_to_all x2 -> x0, local copies, waits for them, and re-layouts: 33.8 us -> none  [on_device(): lax.all_to_all(first, 'rs', split_axis=2, concat_axis=1, tiled=True)]
    dot_general x2 -> x0, matrix products: 31.3 us -> none  [the longest x1 17.5 us: on_device(): jnp.dot(flat, panel, preferred_element_type=jnp.float32)]
    reshape x1 -> x0, local copies, waits for them, and re-layouts: 18.5 us -> none  [on_device(): first = first.reshape(pair_rows, block_rows, NORB)]
    unnamed x3 -> x2, local copies, waits for them, and re-layouts: 0.8 us -> 6.88 us
where the time goes in v1:
time: 264 us
  Pallas kernels  195 us (74%)
  waiting for transfers between devices  44.6 us (17%)
  between operations  13.4 us (5%)
  local copies, waits for them, and re-layouts  6.99 us (3%)
  blocking collectives  4.69 us (2%)
    pallas_call x1, Pallas kernels, fused(): pl.pallas_call(functools.partial(fused_kernel, n, group), out_shape=jax.S...  195 us
    all_gather x1, waiting for transfers between devices, on_device(): panel = lax.all_gather(strip, 'rs', axis=0, tiled=True)  44.5 us
    unnamed x2, local copies, waits for them, and re-layouts  6.88 us
  transfers between devices with their start and end apart: 1, of which 1 were waited for; matrix products, arithmetic and copies ran while one was open for 0% of the time, Pallas kernels for 0%

profile of v1, /device:TPU:1, one launch (start us, length us, event | category | flops | bytes accessed | tf_op | source)
XLA Modules:
  0.0 264.2 jit_solution(15637873969243287337)
XLA Ops:
  6.5 0.0 all-gather.3.cloned.1.call-start
  6.5 4.7 %all-gather = bf16[2,448,72]{1,2,0:T(8,128)(2,1)S(1)} all-gather(bf16[1,448,72]{1,2,0:T(8,128)(2,1)} %bitcast.7), channel_id=1, replica_groups=mesh['pq'=2,'rs'=16] {'pq'}, dimensions={0}, use_global_device_ids=true | all-gather | bytes 193536 | tf_op jit(solution)/shard_map/all_gather | solution.py:133
  11.2 0.1 copy.4
  11.3 0.8 reshape.1
  12.1 0.0 all-gather.3.cloned.1.call-update
  12.2 44.5 %all-gather.3.cloned.1.call-done.c_ref = bf16[1152,896]{1,0:T(8,128)(2,1)} async-done(((bf16[72,896]{1,0:T(8,128)(2,1)}), bf16[1152,896]{1,0:T(8,128)(2,1)}) %all-gather.3.cloned.1.call-update) | async-done | bytes 2064400 | tf_op jit(solution)/shard_map/all_gather | solution.py:134
  56.7 194.6 %shard_map.28 = bf16[64,56,896]{2,1,0:T(8,128)(2,1)} custom-call(bf16[64,72,1152]{2,1,0:T(8,128)(2,1)} %x_ref.1, bf16[1152,896]{1,0:T(8,128)(2,1)} %all-gather.3.cloned.1.call-done.c_ref), custom_call_target="tpu_custom_call" | custom-call | flops 16911433728 | bytes 33030144 | tf_op jit(solution)/shard_map/pallas_call | solution.py:108
  251.3 6.1 %copy.6 = bf16[64,56,896]{2,1,0:T(8,128)(2,1)} copy(bf16[64,56,896]{2,1,0:T(8,128)(2,1)} %shard_map.28) | data formatting | bytes 12845056
Async XLA Ops:
  6.5 50.2 %all-gather.3.cloned.1.call-start = ((), (), s32[]{:S(2)}) async-start(), calls=%async_computation | async-start | bytes 2193408 | tf_op jit(solution)/shard_map/all_gather | solution.py:134
Sparse Core Ops, SparseCore 0:
  12.3 44.3 all-gather.2

commit v2 on v1

--- a/solution.py
+++ b/solution.py
@@ -25,15 +25,26 @@
     return second_half(lax.all_to_all(first, "rs", split_axis=2, concat_axis=1, tiled=True), panel)
 
 
-def fused_kernel(n, group, x_ref, c_ref, o_ref, tiles, send, recv, stage, load_sem, send_sem, recv_sem, own_sem, out_sem):
+def fused_kernel(n, group, x_ref, c_ref, o_ref, tiles, parts, panel, send, recv, stage, load_sem, send_sem, recv_sem, own_sem, out_sem, hop_sem, part_sem, local_sem):
     me = lax.axis_index("rs")
+    col = lax.axis_index("pq")
     groups = send.shape[0]
     rows = send.shape[2]
     width = stage.shape[2]
     nbasis = tiles.shape[3]
     half = n // 2
-    far = lax.rem(me // half + 1, 2) * half
-    near = (me // half) * half
+    far_side = lax.rem(me // half + 1, 2)
+    near_side = me // half
+    far = far_side * half
+    near = near_side * half
+    lines = n // 4
+    core = lax.rem(me, 2)
+    y = lax.rem(me // 2, 2)
+    z = me // 4
+    col_too = 1 - col
+
+    def spot(at_z, at_y, at_core):
+        return at_z * 4 + at_y * 2 + at_core
 
     def load(g):
         return pltpu.make_async_copy(x_ref.at[pl.ds(g * group, group)], tiles.at[g % 2], load_sem.at[g % 2])
@@ -61,34 +72,114 @@
         return pltpu.make_async_copy(send.at[g, me], recv.at[g, me], own_sem.at[g])
 
     load(0).start()
+    local = pltpu.make_async_copy(c_ref, parts.at[col, me], local_sem)
+    local.start()
     barrier = pltpu.get_barrier_semaphore()
     for i in range(1, n):
         pl.semaphore_signal(barrier, inc=1, device_id={"rs": lax.rem(me + i, n)}, device_id_type=MESH)
-    pl.semaphore_wait(barrier, n - 1)
+    pl.semaphore_signal(barrier, inc=1, device_id={"pq": col_too}, device_id_type=MESH)
+    pl.semaphore_wait(barrier, n)
+
+    hops = []
+
+    def pass_on(q, r, to, src=None):
+        copy = pltpu.make_async_remote_copy(
+            src_ref=parts.at[q, r] if src is None else src,
+            dst_ref=parts.at[q, r],
+            send_sem=hop_sem.at[len(hops)],
+            recv_sem=part_sem.at[q, r],
+            device_id=to,
+            device_id_type=MESH,
+        )
+        copy.start()
+        hops.append(copy)
+
+    def arrived(q, r):
+        pltpu.make_async_remote_copy(
+            src_ref=parts.at[q, r],
+            dst_ref=parts.at[q, r],
+            send_sem=hop_sem.at[0],
+            recv_sem=part_sem.at[q, r],
+            device_id={"pq": col_too},
+            device_id_type=MESH,
+        ).wait_recv()
+
+    across_y = {"rs": spot(z, 1 - y, core)}
+    across_x = {"pq": col_too}
+    across_core = {"rs": spot(z, y, 1 - core)}
+    for k in range(1, lines):
+        pass_on(col, me, {"rs": spot(lax.rem(z + k, lines), y, core)}, c_ref)
+    for k in range(lines):
+        r = spot(lax.rem(z + lines - k, lines), y, core)
+        if k:
+            arrived(col, r)
+        src = None if k else c_ref
+        pass_on(col, r, across_y, src)
+        pass_on(col, r, across_x, src)
+        pass_on(col, r, across_core, src)
+    for k in range(lines):
+        at_z = lax.rem(z + lines - k, lines)
+        mine, other = spot(at_z, y, core), spot(at_z, 1 - y, core)
+        arrived(col_too, mine)
+        arrived(col, other)
+        if k % 2:
+            pass_on(col, other, across_x)
+        else:
+            pass_on(col_too, mine, across_y)
+        pass_on(col_too, mine, across_core)
+        pass_on(col, other, across_core)
+    for k in range(lines):
+        other = spot(lax.rem(z + lines - k, lines), 1 - y, core)
+        arrived(col_too, other)
+        pass_on(col_too, other, across_core)
+    for k in range(lines):
+        for q in (col, col_too):
+            for at_y in (0, 1):
+                arrived(q, spot(k, at_y, 1 - core))
+    local.wait()
 
     step = 4
     for g in range(groups):
         if g + 1 < groups:
             load(g + 1).start()
         load(g).wait()
-        for q in range(group // step):
-            block = tiles[g % 2, q * step : (q + 1) * step].reshape(step * rows, nbasis)
-            first = jnp.dot(block, c_ref[...], preferred_element_type=jnp.float32)
-            for j in range(step):
-                slot = q * step + j
-                piece = first[j * rows : (j + 1) * rows].astype(jnp.bfloat16)
-                for d in range(n):
-                    send[g, d, :, slot * width : (slot + 1) * width] = piece[:, d * width : (d + 1) * width]
-        for i in range(n - 1):
-            remote(g, i).start()
+        for side in (0, 1):
+            weights = parts[near_side if side else far_side].reshape(nbasis, half * width)
+            base = near if side else far
+            for q in range(group // step):
+                block = tiles[g % 2, q * step : (q + 1) * step].reshape(step * rows, nbasis)
+                first = jnp.dot(block, weights, preferred_element_type=jnp.float32)
+                for j in range(step):
+                    slot = q * step + j
+                    piece = first[j * rows : (j + 1) * rows].astype(jnp.bfloat16)
+                    for d in range(half):
+                        send[g, base + d, :, slot * width : (slot + 1) * width] = piece[:, d * width : (d + 1) * width]
+            for i in range(half, n - 1) if side else range(half):
+                remote(g, i).start()
         own(g).start()
 
+    for q in (0, 1):
+        panel[:, q * half * width : (q + 1) * half * width] = parts[q].reshape(nbasis, half * width)
+    for copy in hops:
+        copy.wait_send()
+
+    contract = (((0,), (0,)), ((), ()))
     for g in range(groups):
         own(g).wait()
-        for i in range(n - 1):
-            remote(g, i).wait()
-        lhs = recv[g].reshape(n * rows, group * width)
-        out = lax.dot_general(lhs, c_ref[...], (((0,), (0,)), ((), ())), preferred_element_type=jnp.float32)
+        if g + 1 < groups:
+            for i in range(n - 1):
+                remote(g, i).wait()
+            lhs = recv[g].reshape(n * rows, group * width)
+            out = lax.dot_general(lhs, panel[...], contract, preferred_element_type=jnp.float32)
+        else:
+            out = 0.0
+            for side in (1, 0):
+                base = near if side else far
+                for i in range(half, n - 1) if side else range(half):
+                    remote(g, i).wait()
+                lhs = recv[g, pl.ds(base, half)].reshape(half * rows, group * width)
+                part = panel[pl.ds(pl.multiple_of(base * rows, 16), half * rows)]
+                out += lax.dot_general(lhs, part, contract, preferred_element_type=jnp.float32)
         if g >= 2:
             store(g - 2).wait()
         for j in range(group):
@@ -98,9 +189,10 @@
         store(g).wait()
 
 
-def fused(n, group, integrals, panel):
+def fused(n, group, integrals, coeff):
     pair_rows, rows, nbasis = integrals.shape
-    norb = panel.shape[1]
+    columns = coeff.shape[1]
+    norb = 2 * columns
     width = norb // n
     groups = pair_rows // group
     flops = 2 * pair_rows * rows * nbasis * norb + 2 * pair_rows * width * n * rows * norb
@@ -112,6 +204,8 @@
         out_specs=pl.BlockSpec(memory_space=pl.ANY),
         scratch_shapes=[
             pltpu.VMEM((2, group, rows, nbasis), jnp.bfloat16),
+            pltpu.VMEM((2, n, rows, columns), jnp.bfloat16),
+            pltpu.VMEM((nbasis, norb), jnp.bfloat16),
             pltpu.VMEM((groups, n, rows, group * width), jnp.bfloat16),
             pltpu.VMEM((groups, n, rows, group * width), jnp.bfloat16),
             pltpu.VMEM((2, group, width, norb), jnp.bfloat16),
@@ -120,29 +214,33 @@
             pltpu.SemaphoreType.DMA((groups, n)),
             pltpu.SemaphoreType.DMA((groups,)),
             pltpu.SemaphoreType.DMA((2,)),
+            pltpu.SemaphoreType.DMA((2 * n,)),
+            pltpu.SemaphoreType.DMA((2, n)),
+            pltpu.SemaphoreType.DMA,
         ],
         compiler_params=pltpu.CompilerParams(
             collective_id=0, has_side_effects=True, vmem_limit_bytes=60 * 2**20
         ),
         cost_estimate=pl.CostEstimate(flops=flops, bytes_accessed=4 * sent, transcendentals=0),
-    )(integrals, panel)
-
-
-def on_device(n, integrals, coeff):
+    )(integrals, coeff)
+
+
+def on_device(n, splits, integrals, coeff):
     pair_rows, rows, nbasis = integrals.shape
+    norb = coeff.shape[1] * splits
+    width = norb // n
+    group = math.lcm(4, 128 // math.gcd(width, 128))
+    aligned = rows % 8 == 0 and width % 8 == 0 and pair_rows % group == 0 and n * rows % 32 == 0
+    if splits == 2 and n % 4 == 0 and aligned and group * width <= 2048:
+        return fused(n, group, integrals, coeff)
     strip = lax.all_gather(coeff, "pq", axis=1, tiled=True)
-    panel = lax.all_gather(strip, "rs", axis=0, tiled=True)
-    width = panel.shape[1] // n
-    group = math.lcm(4, 128 // math.gcd(width, 128))
-    if rows % 8 or width % 8 or n % 2 or pair_rows % group or group * width > 2048:
-        return plain(integrals, panel)
-    return fused(n, group, integrals, panel)
+    return plain(integrals, lax.all_gather(strip, "rs", axis=0, tiled=True))
 
 
 def solution(mesh):
     placed = (P("pq", "rs", None), P("rs", "pq"))
     return jax.shard_map(
-        functools.partial(on_device, mesh.shape["rs"]),
+        functools.partial(on_device, mesh.shape["rs"], mesh.shape["pq"]),
         mesh=mesh,
         in_specs=placed,
         out_specs=P("pq", "rs", None),

time: 264 us -> 222 us (0.84)
  waiting for transfers between devices: 44.6 us -> 0 us
  Pallas kernels: 195 us -> 216 us
  between operations: 13.4 us -> 0.01 us
  blocking collectives: 4.69 us -> 0 us
    all_gather x1 -> x0, waiting for transfers between devices: 44.5 us -> none  [on_device(): panel = lax.all_gather(strip, 'rs', axis=0, tiled=True)]
    pallas_call x1, Pallas kernels: 195 us -> 216 us  [fused(): pl.pallas_call(functools.partial(fused_kernel, n, group), out_shape=jax.S...]
    all_gather x1 -> x0, blocking collectives: 4.69 us -> none  [on_device(): strip = lax.all_gather(coeff, 'pq', axis=1, tiled=True)]
    unnamed x2 -> x1, local copies, waits for them, and re-layouts: 6.88 us -> 6.08 us
  transfers between devices with their start and end apart: 1 -> 0, of which waited for: 1 -> 0; matrix products, arithmetic and copies ran while one was open for 0% -> 0% of each run, Pallas kernels for 0% -> 0%
where the time goes in v2:
time: 222 us
  Pallas kernels  216 us (97%)
  local copies, waits for them, and re-layouts  6.08 us (3%)
    pallas_call x1, Pallas kernels, fused(): pl.pallas_call(functools.partial(fused_kernel, n, group), out_shape=jax.S...  216 us
    unnamed x1, local copies, waits for them, and re-layouts  6.08 us

profile of v2, /device:TPU:1, one launch (start us, length us, event | category | flops | bytes accessed | tf_op | source)
XLA Modules:
  0.0 222.0 jit_solution(16419692712018577522)
XLA Ops:
  0.0 215.9 %shard_map.28 = bf16[64,56,896]{2,1,0:T(8,128)(2,1)} custom-call(bf16[64,72,1152]{2,1,0:T(8,128)(2,1)} %x_ref.1, bf16[72,448]{1,0:T(8,128)(2,1)} %c_ref.1), custom_call_target="tpu_custom_call" | custom-call | flops 16911433728 | bytes 33030144 | tf_op jit(solution)/shard_map/pallas_call | solution.py:200
  215.9 6.1 %copy.4 = bf16[64,56,896]{2,1,0:T(8,128)(2,1)} copy(bf16[64,56,896]{2,1,0:T(8,128)(2,1)} %shard_map.28) | data formatting | bytes 12845056

commit v3 on v2

--- a/solution.py
+++ b/solution.py
@@ -54,16 +54,23 @@
 
     def partner(i):
         if i < half:
-            return far + lax.rem(me + i, half)
+            pair = lax.rem(lax.rem(me, half) // 2 + i // 2, half // 2)
+            return far + pair * 2 + lax.rem(me + i, 2)
         return near + lax.rem(me + i - half + 1, half)
 
-    def remote(g, i):
+    cuts = 3 if rows % 24 == 0 else 1
+    short = rows // cuts
+
+    def remote(g, i, cut=None):
         to = partner(i)
+        first_cut = g == 0 and i < half
+        some = pl.ds((cut or 0) * short, short) if first_cut else pl.ds(0, rows)
+        sem = groups + cut - 1 if first_cut and cut else g
         return pltpu.make_async_remote_copy(
-            src_ref=send.at[g, to],
-            dst_ref=recv.at[g, me],
-            send_sem=send_sem.at[g, i],
-            recv_sem=recv_sem.at[g, i],
+            src_ref=send.at[g, to, some],
+            dst_ref=recv.at[g, me, some],
+            send_sem=send_sem.at[sem, i],
+            recv_sem=recv_sem.at[sem, i],
             device_id={"rs": to},
             device_id_type=MESH,
         )
@@ -109,34 +116,38 @@
     across_core = {"rs": spot(z, y, 1 - core)}
     for k in range(1, lines):
         pass_on(col, me, {"rs": spot(lax.rem(z + k, lines), y, core)}, c_ref)
-    for k in range(lines):
-        r = spot(lax.rem(z + lines - k, lines), y, core)
-        if k:
-            arrived(col, r)
-        src = None if k else c_ref
-        pass_on(col, r, across_y, src)
-        pass_on(col, r, across_x, src)
-        pass_on(col, r, across_core, src)
-    for k in range(lines):
-        at_z = lax.rem(z + lines - k, lines)
-        mine, other = spot(at_z, y, core), spot(at_z, 1 - y, core)
-        arrived(col_too, mine)
-        arrived(col, other)
-        if k % 2:
-            pass_on(col, other, across_x)
-        else:
-            pass_on(col_too, mine, across_y)
-        pass_on(col_too, mine, across_core)
-        pass_on(col, other, across_core)
-    for k in range(lines):
-        other = spot(lax.rem(z + lines - k, lines), 1 - y, core)
-        arrived(col_too, other)
-        pass_on(col_too, other, across_core)
-    for k in range(lines):
-        for q in (col, col_too):
+    def along(k):
+        return lax.rem(z + lines - k, lines)
+
+    for k in range(lines + 2):
+        if k < lines:
+            r = spot(along(k), y, core)
+            if k:
+                arrived(col, r)
+            src = None if k else c_ref
+            pass_on(col, r, across_y, src)
+            pass_on(col, r, across_x, src)
+            pass_on(col, r, across_core, src)
+        if 0 <= k - 1 < lines:
+            mine, other = spot(along(k - 1), y, core), spot(along(k - 1), 1 - y, core)
+            arrived(col_too, mine)
+            arrived(col, other)
+            if (k - 1) % 2:
+                pass_on(col, other, across_x)
+            else:
+                pass_on(col_too, mine, across_y)
+            pass_on(col_too, mine, across_core)
+            pass_on(col, other, across_core)
+        if 0 <= k - 2:
+            other = spot(along(k - 2), 1 - y, core)
+            arrived(col_too, other)
+            pass_on(col_too, other, across_core)
+    local.wait()
+
+    def arrived_from_core(q):
+        for k in range(lines):
             for at_y in (0, 1):
                 arrived(q, spot(k, at_y, 1 - core))
-    local.wait()
 
     step = 4
     for g in range(groups):
@@ -144,8 +155,21 @@
             load(g + 1).start()
         load(g).wait()
         for side in (0, 1):
+            if g == 0:
+                arrived_from_core(near_side if side else far_side)
             weights = parts[near_side if side else far_side].reshape(nbasis, half * width)
             base = near if side else far
+            if g == 0 and side == 0:
+                for cut in range(cuts):
+                    block = tiles[0, :, cut * short : (cut + 1) * short].reshape(group * short, nbasis)
+                    first = jnp.dot(block, weights, preferred_element_type=jnp.float32)
+                    for slot in range(group):
+                        piece = first[slot * short : (slot + 1) * short].astype(jnp.bfloat16)
+                        for d in range(half):
+                            send[0, base + d, cut * short : (cut + 1) * short, slot * width : (slot + 1) * width] = piece[:, d * width : (d + 1) * width]
+                    for i in range(half):
+                        remote(0, i, cut).start()
+                continue
             for q in range(group // step):
                 block = tiles[g % 2, q * step : (q + 1) * step].reshape(step * rows, nbasis)
                 first = jnp.dot(block, weights, preferred_element_type=jnp.float32)
@@ -168,17 +192,24 @@
         own(g).wait()
         if g + 1 < groups:
             for i in range(n - 1):
-                remote(g, i).wait()
+                for cut in range(cuts if g == 0 and i < half else 1):
+                    remote(g, i, cut).wait()
             lhs = recv[g].reshape(n * rows, group * width)
             out = lax.dot_general(lhs, panel[...], contract, preferred_element_type=jnp.float32)
         else:
+            for i in range(half, n - 1):
+                remote(g, i).wait()
+            chunks = [(near, half)]
+            for a in range(half // 2):
+                pair = lax.rem(lax.rem(me, half) // 2 + half // 2 - a, half // 2)
+                chunks.append((far + 2 * pair, 2))
             out = 0.0
-            for side in (1, 0):
-                base = near if side else far
-                for i in range(half, n - 1) if side else range(half):
-                    remote(g, i).wait()
-                lhs = recv[g, pl.ds(base, half)].reshape(half * rows, group * width)
-                part = panel[pl.ds(pl.multiple_of(base * rows, 16), half * rows)]
+            for at, (base, count) in enumerate(chunks):
+                if at:
+                    remote(g, 2 * at - 2).wait()
+                    remote(g, 2 * at - 1).wait()
+                lhs = recv[g, pl.ds(base, count)].reshape(count * rows, group * width)
+                part = panel[pl.ds(pl.multiple_of(base * rows, 16), count * rows)]
                 out += lax.dot_general(lhs, part, contract, preferred_element_type=jnp.float32)
         if g >= 2:
             store(g - 2).wait()
@@ -210,8 +241,8 @@
             pltpu.VMEM((groups, n, rows, group * width), jnp.bfloat16),
             pltpu.VMEM((2, group, width, norb), jnp.bfloat16),
             pltpu.SemaphoreType.DMA((2,)),
-            pltpu.SemaphoreType.DMA((groups, n)),
-            pltpu.SemaphoreType.DMA((groups, n)),
+            pltpu.SemaphoreType.DMA((groups + 2, n)),
+            pltpu.SemaphoreType.DMA((groups + 2, n)),
             pltpu.SemaphoreType.DMA((groups,)),
             pltpu.SemaphoreType.DMA((2,)),
             pltpu.SemaphoreType.DMA((2 * n,)),
@@ -230,7 +261,7 @@
     norb = coeff.shape[1] * splits
     width = norb // n
     group = math.lcm(4, 128 // math.gcd(width, 128))
-    aligned = rows % 8 == 0 and width % 8 == 0 and pair_rows % group == 0 and n * rows % 32 == 0
+    aligned = rows % 8 == 0 and width % 8 == 0 and pair_rows % group == 0 and pair_rows >= 2 * group
     if splits == 2 and n % 4 == 0 and aligned and group * width <= 2048:
         return fused(n, group, integrals, coeff)
     strip = lax.all_gather(coeff, "pq", axis=1, tiled=True)

time: 222 us -> 216 us (0.973)
  Pallas kernels: 216 us -> 208 us
    pallas_call x1, Pallas kernels: 216 us -> 208 us  [fused(): pl.pallas_call(functools.partial(fused_kernel, n, group), out_shape=jax.S...]
where the time goes in v3:
time: 216 us; the launch traced here: 214 us
  Pallas kernels  208 us (96%)
  local copies, waits for them, and re-layouts  6.08 us (3%)
    pallas_call x1, Pallas kernels, fused(): pl.pallas_call(functools.partial(fused_kernel, n, group), out_shape=jax.S...  208 us
    unnamed x1, local copies, waits for them, and re-layouts  6.08 us

profile of v3, /device:TPU:1, one launch (start us, length us, event | category | flops | bytes accessed | tf_op | source)
XLA Modules:
  0.0 214.2 jit_solution(8157722445056937130)
XLA Ops:
  0.0 208.1 %shard_map.28 = bf16[64,56,896]{2,1,0:T(8,128)(2,1)} custom-call(bf16[64,72,1152]{2,1,0:T(8,128)(2,1)} %x_ref.1, bf16[72,448]{1,0:T(8,128)(2,1)} %c_ref.1), custom_call_target="tpu_custom_call" | custom-call | flops 16911433728 | bytes 33030144 | tf_op jit(solution)/shard_map/pallas_call | solution.py:231
  208.1 6.1 %copy.4 = bf16[64,56,896]{2,1,0:T(8,128)(2,1)} copy(bf16[64,56,896]{2,1,0:T(8,128)(2,1)} %shard_map.28) | data formatting | bytes 12845056
